TPU v7x, 32 devices: a whole 2x2x4 slice. The times are simulated.
32 devices in a mesh: dp: 8 (over z, x), mp: 4 (over y, core).
Axes of the slice: x: 2, y: 2, z: 4, core: 2. Of those that a mesh axis runs over, the one named last changes fastest.
Arguments:
- vlm_tokens: bfloat16 [2048, 2048], P(('dp', 'mp')), may hold values from -64 to 64
- action_tokens: bfloat16 [4096, 2048], P(('dp', 'mp')), may hold values from -64 to 64
- norm_gain: float32 [2048], replicated, may hold values from 0.25 to 1.75
- proj_old: bfloat16 [4096, 4096], P('dp', 'mp'), may hold values from -0.125 to 0.125
Outputs:
- vlm_hidden: bfloat16 [4096, 4096], P('dp', 'mp')
- action_hidden: bfloat16 [4096, 8192], P('dp', 'mp')
- proj_new: bfloat16 [2048, 8192], P('dp', 'mp')
All inputs are finite; a program needn't handle non-finite values.
Results may differ from a plain program's by a relative error of at most 0.005.
Values may be sent and summed in bfloat16 or wider, within the bound.
A program may use at most 64 MiB of HBM per device.

v0:
```python
import jax
import jax.numpy as jnp
from jax import lax
from jax.sharding import PartitionSpec as P

epsilon = 1e-06


def partner(array, axis, apart):
    return lax.ppermute(array, axis, [(i, i ^ 1 << apart) for i in range(lax.axis_size(axis))])


def normalize(row_values, norm_gain):
    values = row_values.astype(jnp.float32)
    factor = lax.rsqrt(jnp.mean(values * values, axis=-1, keepdims=True) + epsilon)
    return (values * factor * norm_gain).astype(jnp.bfloat16)


def ordered(parity, own_part, other_part, axis_number):
    leading = jnp.where(parity == 0, own_part, other_part)
    trailing = jnp.where(parity == 0, other_part, own_part)
    return jnp.concatenate([leading, trailing], axis_number)


def local(vlm_tokens, action_tokens, norm_gain, proj_old):
    parity = lax.axis_index("dp") % 2
    row_half = proj_old.shape[0] // 2
    col_block = proj_old.shape[1]
    kept_rows = lax.dynamic_slice_in_dim(proj_old, parity * row_half, row_half, 0)
    given_rows = lax.dynamic_slice_in_dim(proj_old, (1 - parity) * row_half, row_half, 0)
    taken_rows = partner(given_rows, "dp", 0)
    proj_new = ordered(parity, kept_rows, taken_rows, 1)
    own_group = lax.all_gather(vlm_tokens, "mp", axis=0, tiled=True)
    other_group = partner(own_group, "dp", 0)
    group_rows = ordered(parity, own_group, other_group, 0)
    normed_vlm = normalize(group_rows, norm_gain)
    action_rows = lax.all_gather(action_tokens, "mp", axis=0, tiled=True)
    normed_action = normalize(action_rows, norm_gain)
    new_rows = proj_new.shape[0]
    halves = jnp.stack([proj_new[:, :col_block], proj_new[:, col_block:]])
    tiled_halves = jnp.broadcast_to(
        halves[None], (lax.axis_size("dp") // 2, 2, new_rows, col_block)
    ).reshape(lax.axis_size("dp"), new_rows, col_block)
    received = lax.all_to_all(tiled_halves, "dp", split_axis=0, concat_axis=0, tiled=True)
    own_weight = received.reshape(-1, col_block)
    vlm_pre = jnp.dot(normed_vlm, own_weight, preferred_element_type=jnp.float32)
    vlm_hidden = jax.nn.gelu(vlm_pre, approximate=False).astype(jnp.bfloat16)
    partner_normed = partner(normed_action, "dp", 0)
    both_rows = jnp.concatenate([normed_action, partner_normed], 0)
    both_pre = jnp.dot(both_rows, own_weight, preferred_element_type=jnp.float32)
    both_hidden = jax.nn.gelu(both_pre, approximate=False).astype(jnp.bfloat16)
    action_count = normed_action.shape[0]
    mine = both_hidden[:action_count]
    from_partner = partner(both_hidden[action_count:], "dp", 0)
    action_hidden = ordered(parity, mine, from_partner, 1)
    return (vlm_hidden, action_hidden, proj_new)


def solution(mesh):
    return jax.shard_map(
        local,
        mesh=mesh,
        in_specs=(P(("dp", "mp"), None), P(("dp", "mp"), None), P(), P("dp", "mp")),
        out_specs=(P("dp", "mp"), P("dp", "mp"), P("dp", "mp")),
        check_vma=False,
    )
```

profile of v0, /device:TPU:0, one launch (start us, length us, event | category | flops | bytes accessed | tf_op | source)
XLA Modules:
  0.0 210.4 jit_solution(8145602207031625313)
XLA Ops:
  7.2 1.1 constant_dynamic-slice_fusion
  8.3 3.0 %collective-permute-start.1 = (bf16[256,1024]{1,0:T(8,128)(2,1)S(1)}, bf16[256,1024]{1,0:T(8,128)(2,1)S(1)}, u32[]{:S(2)}, u32[]{:S(2)}) collective-permute-start(bf16[256,1024]{1,0:T(8,128)(2,1)S(1)} %constant_dynamic-slice_fusion), channel_id=1, source_target_pairs={{0,4},{4,0},{8,12},{12,8},{16,20},{20,16},{24,28},{28,24},{1,5},{5... | collective-permute-start | bytes 1572872 | tf_op jit(solution)/shard_map/ppermute | solution.py:10
  11.3 11.9 %collective-permute-done.1 = bf16[256,1024]{1,0:T(8,128)(2,1)S(1)} collective-permute-done((bf16[256,1024]{1,0:T(8,128)(2,1)S(1)}, bf16[256,1024]{1,0:T(8,128)(2,1)S(1)}, u32[]{:S(2)}, u32[]{:S(2)}) %collective-permute-start.1) | collective-permute-done | bytes 524320 | tf_op jit(solution)/shard_map/ppermute | solution.py:10
  23.2 1.3 broadcast_select_fusion.5
  24.5 0.1 pad_maximum_fusion.3
  24.6 2.5 %broadcast_in_dim.2 = bf16[4,2,256,1024]{3,2,1,0:T(8,128)(2,1)} broadcast(bf16[2,256,1024]{2,1,0:T(8,128)(2,1)S(1)} %pad_maximum_fusion.3), dimensions={1,2,3} | broadcast | bytes 5242880 | tf_op jit(solution)/shard_map/broadcast_in_dim | solution.py:41
  27.1 0.0 copy-start
  27.1 6.2 %all-to-all-start = ((bf16[8,256,1024]{2,1,0:T(8,128)(2,1)}), bf16[8,256,1024]{2,1,0:T(8,128)(2,1)}, u32[]{:S(2)}, u32[]{:S(2)}) async-start(bf16[8,256,1024]{2,1,0:T(8,128)(2,1)} %bitcast.6), calls=%async_computation | async-start | bytes 8388608 | tf_op jit(solution)/shard_map/all_to_all | solution.py:44
  33.3 0.0 all-gather.5.cloned.1.call-start
  33.4 0.7 all-gather.5.cloned.1.call-update
  34.1 0.0 all-gather.3.cloned.1.call-start
  34.1 0.7 all-gather.3.cloned.1.call-update
  34.8 24.9 %all-gather.5.cloned.1.call-done = bf16[512,2048]{1,0:T(8,128)(2,1)} async-done(((bf16[128,2048]{1,0:T(8,128)(2,1)}), bf16[512,2048]{1,0:T(8,128)(2,1)}) %all-gather.5.cloned.1.call-update) | async-done | bytes 2097168 | tf_op jit(solution)/shard_map/all_gather | solution.py:37
  59.7 2.1 fusion.3
  61.8 0.0 copy-done
  61.8 3.5 %fusion.5 = bf16[512,2048]{1,0:T(8,128)(2,1)} fusion(bf16[512,2048]{1,0:T(8,128)(2,1)} %all-gather.5.cloned.1.call-done, f32[512]{0:T(512)S(1)} %add_rsqrt_fusion, f32[2048]{0:T(1024)S(1)} %copy-done), kind=kLoop, calls=%fused_computation.10 | loop fusion | flops 4194304 | bytes 4204544 | tf_op jit(solution)/shard_map/convert_element_type | solution.py:16
  65.3 1.5 collective-permute-start.2
  66.7 11.3 %all-gather.3.cloned.1.call-done = bf16[256,2048]{1,0:T(8,128)(2,1)} async-done(((bf16[64,2048]{1,0:T(8,128)(2,1)}), bf16[256,2048]{1,0:T(8,128)(2,1)}) %all-gather.3.cloned.1.call-update) | async-done | bytes 1048592 | tf_op jit(solution)/shard_map/all_gather | solution.py:33
  78.0 1.5 collective-permute-start
  79.5 1.1 pad_maximum_fusion.4
  80.5 75.7 %collective-permute-done = bf16[256,2048]{1,0:T(8,128)(2,1)S(1)} collective-permute-done((bf16[256,2048]{1,0:T(8,128)(2,1)}, bf16[256,2048]{1,0:T(8,128)(2,1)S(1)}, u32[]{:S(2)}, u32[]{:S(2)}) %collective-permute-start) | collective-permute-done | bytes 1048608 | tf_op jit(solution)/shard_map/ppermute | solution.py:10
  156.2 1.4 broadcast_select_fusion.3
  157.6 0.5 fusion
  158.1 0.0 collective-permute-done.2
  158.1 0.0 all-to-all-done
  158.1 18.1 %fusion.8 = bf16[1024,1024]{0,1:T(8,128)(2,1)S(1)} fusion(bf16[2048,1024]{1,0:T(8,128)(2,1)} %bitcast.3, bf16[512,2048]{1,0:T(8,128)(2,1)} %collective-permute-done.2, bf16[512,2048]{1,0:T(8,128)(2,1)} %fusion.5), kind=kOutput, calls=%fused_computation.13 | convolution fusion | flops 4371513344 | bytes 10485760 | tf_op jit(solution)/shard_map/dot_general | solution.py:50
  176.2 0.1 slice.9
  176.4 0.1 collective-permute-start.3
  176.4 9.8 %fusion.24 = bf16[512,1024]{1,0:T(8,128)(2,1)} fusion(bf16[2048,1024]{1,0:T(8,128)(2,1)} %bitcast.3, f32[2048]{0:T(1024)S(1)} %copy-done, f32[512]{0:T(512)S(1)} %add_rsqrt_fusion.1, bf16[256,2048]{1,0:T(8,128)(2,1)S(1)} %get-tuple-element.9, bf16[256,2048]{1,0:T(8,128)(2,1)S(1)} %get-tuple-element.8), kind=kOutput, calls=%fused_computation.36 | convolution fusion | flops 2188902400 | bytes 7350272 | tf_op jit(solution)/shard_map/dot_general | solution.py:46
  186.2 14.6 %collective-permute-done.3 = bf16[512,1024]{0,1:T(8,128)(2,1)S(1)} collective-permute-done((bf16[512,1024]{0,1:T(8,128)(2,1)S(1)}, bf16[512,1024]{0,1:T(8,128)(2,1)S(1)}, u32[]{:S(2)}, u32[]{:S(2)}) %collective-permute-start.3) | collective-permute-done | bytes 1048608 | tf_op jit(solution)/shard_map/ppermute | solution.py:10
  200.9 0.2 broadcast_select_fusion.1
  201.1 0.1 pad_maximum_fusion.1
  201.2 2.4 %copy.7 = bf16[512,2048]{1,0:T(8,128)(2,1)} copy(bf16[512,2048]{0,1:T(8,128)(2,1)S(1)} %pad_maximum_fusion.1) | data formatting | bytes 4194304
  (2 shorter events, 0.0 us)
Async XLA Ops:
  8.3 15.0 %collective-permute-start.1 = (bf16[256,1024]{1,0:T(8,128)(2,1)S(1)}, bf16[256,1024]{1,0:T(8,128)(2,1)S(1)}, u32[]{:S(2)}, u32[]{:S(2)}) collective-permute-start(bf16[256,1024]{1,0:T(8,128)(2,1)S(1)} %constant_dynamic-slice_fusion), channel_id=1, source_target_pairs={{0,4},{4,0},{8,12},{12,8},{16,20},{20,16},{24,28},{28,24},{1,5},{5... | collective-permute-start | bytes 1572872 | tf_op jit(solution)/shard_map/ppermute | solution.py:10
  27.1 34.7 %copy-start = (f32[2048]{0:T(1024)S(1)}, f32[2048]{0:T(1024)}, u32[]{:S(2)}) copy-start(f32[2048]{0:T(1024)} %param.6) | copy-start | bytes 24580
  27.1 131.0 %all-to-all-start = ((bf16[8,256,1024]{2,1,0:T(8,128)(2,1)}), bf16[8,256,1024]{2,1,0:T(8,128)(2,1)}, u32[]{:S(2)}, u32[]{:S(2)}) async-start(bf16[8,256,1024]{2,1,0:T(8,128)(2,1)} %bitcast.6), calls=%async_computation | async-start | bytes 8388608 | tf_op jit(solution)/shard_map/all_to_all | solution.py:44
  33.3 26.4 %all-gather.5.cloned.1.call-start = ((), (), s32[]{:S(2)}) async-start(), calls=%async_computation.2 | async-start | bytes 2621440 | tf_op jit(solution)/shard_map/all_gather | solution.py:37
  34.1 44.0 %all-gather.3.cloned.1.call-start = ((), (), s32[]{:S(2)}) async-start(), calls=%async_computation.1 | async-start | bytes 1310720 | tf_op jit(solution)/shard_map/all_gather | solution.py:33
  65.3 92.8 %collective-permute-start.2 = (bf16[512,2048]{1,0:T(8,128)(2,1)}, bf16[512,2048]{1,0:T(8,128)(2,1)}, u32[]{:S(2)}, u32[]{:S(2)}) collective-permute-start(bf16[512,2048]{1,0:T(8,128)(2,1)} %fusion.5), channel_id=1, source_target_pairs={{0,4},{4,0},{8,12},{12,8},{16,20},{20,16},{24,28},{28,24},{1,5},{5... | collective-permute-start | bytes 6291464 | tf_op jit(solution)/shard_map/ppermute | solution.py:10
  78.0 78.2 %collective-permute-start = (bf16[256,2048]{1,0:T(8,128)(2,1)}, bf16[256,2048]{1,0:T(8,128)(2,1)S(1)}, u32[]{:S(2)}, u32[]{:S(2)}) collective-permute-start(bf16[256,2048]{1,0:T(8,128)(2,1)} %all-gather.3.cloned.1.call-done), channel_id=1, source_target_pairs={{0,4},{4,0},{8,12},{12,8},{16,20},{20,16},{24,28},{28,24},{1,5},{5... | collective-permute-start | bytes 3145736 | tf_op jit(solution)/shard_map/ppermute | solution.py:10
  176.4 24.5 %collective-permute-start.3 = (bf16[512,1024]{0,1:T(8,128)(2,1)S(1)}, bf16[512,1024]{0,1:T(8,128)(2,1)S(1)}, u32[]{:S(2)}, u32[]{:S(2)}) collective-permute-start(bf16[512,1024]{0,1:T(8,128)(2,1)S(1)} %slice.9), channel_id=1, source_target_pairs={{0,4},{4,0},{8,12},{12,8},{16,20},{20,16},{24,28},{28,24},{1,5},{5... | collective-permute-start | bytes 3145736 | tf_op jit(solution)/shard_map/ppermute | solution.py:10
Sparse Core Ops, SparseCore 0:
  35.7 23.9 all-gather.4
  61.3 16.6 all-gather.2
where the time goes:
time: 211 us; the launch traced here: 210 us
  waiting for transfers between devices  140 us (66%)
  matrix products  27.9 us (13%)
  between operations  14.1 us (7%)
  starting transfers between devices  12.3 us (6%)
  other arithmetic  10.2 us (5%)
  local copies, waits for them, and re-layouts  6.07 us (3%)
    ppermute x4, waiting for transfers between devices, partner(): lax.ppermute(array, axis, [(i, i ^ 1 << apart) for i in range(lax.axis_si...  102 us
    all_gather x1, waiting for transfers between devices, local(): action_rows = lax.all_gather(action_tokens, 'mp', axis=0, tiled=True)  24.9 us
    dot_general x1, matrix products, local(): jnp.dot(both_rows, own_weight, preferred_element_type=jnp.float32)  18.1 us
    all_gather x1, waiting for transfers between devices, local(): own_group = lax.all_gather(vlm_tokens, 'mp', axis=0, tiled=True)  11.3 us
    dot_general x1, matrix products, local(): jnp.dot(normed_vlm, own_weight, preferred_element_type=jnp.float32)  9.78 us
    all_to_all x1, starting transfers between devices, local(): lax.all_to_all(tiled_halves, 'dp', split_axis=0, concat_axis=0, tiled=True)  6.19 us
    ppermute x4, starting transfers between devices, partner(): lax.ppermute(array, axis, [(i, i ^ 1 << apart) for i in range(lax.axis_si...  6.04 us
  transfers between devices with their start and end apart: 7, of which 5 were waited for; matrix products, arithmetic and copies ran while one was open for 9% of the time, Pallas kernels for 0%

commit v1 on v0

v1 whole, which is shorter than its diff:
```python
import functools
import math
import jax
import jax.numpy as jnp
from jax import lax
from jax.experimental import pallas as pl
from jax.experimental.pallas import tpu as pltpu
from jax.sharding import PartitionSpec as P

MESH = pl.DeviceIdType.MESH
epsilon = 1e-06
CHUNKS = 4


def normalize(row_values, norm_gain):
    values = row_values.astype(jnp.float32)
    factor = lax.rsqrt(jnp.mean(values * values, axis=-1, keepdims=True) + epsilon)
    return (values * factor * norm_gain).astype(jnp.bfloat16)


def gelu(u):
    return (u * 0.5 * (1.0 + lax.erf(u * math.sqrt(0.5)))).astype(jnp.bfloat16)


def kernel(groups, mp_size, chunks, vlm_ref, act_ref, gain_ref, proj_ref, vlm_out, act_out, new_out,
           tok, wbuf, hid, tok_send, tok_recv, w_send, w_recv, ex_send, ex_recv, hid_send, hid_recv, loc):
    d = lax.axis_index("dp")
    m = lax.axis_index("mp")
    g, p = d // 2, d % 2
    y, c = m // 2, m % 2
    vr, ar = vlm_ref.shape[0], act_ref.shape[0]
    r, cols = proj_ref.shape
    half = r // 2
    cw = cols // chunks
    vlm_rows, act_rows = 2 * mp_size * vr, mp_size * ar
    sibling = (d, y * 2 + 1 - c)
    xpart = (g * 2 + 1 - p, m)
    ypart = (d, (1 - y) * 2 + c)
    has_left, has_right = g > 0, g < groups - 1

    barrier = pltpu.get_barrier_semaphore()
    for other in (sibling, xpart, ypart):
        pl.semaphore_signal(barrier, inc=1, device_id=other, device_id_type=MESH)

    @pl.when(has_left)
    def _():
        pl.semaphore_signal(barrier, inc=1, device_id=(d - 2, m), device_id_type=MESH)

    @pl.when(has_right)
    def _():
        pl.semaphore_signal(barrier, inc=1, device_id=(d + 2, m), device_id_type=MESH)

    def load_w():
        return pltpu.make_async_copy(proj_ref, wbuf.at[pl.ds(pl.multiple_of(g * r, r), r), :], loc.at[0])

    load_w().start()

    def place(pp, mm):
        s = pp * mp_size + mm
        return (pl.ds(pl.multiple_of(s * vr, vr), vr), pl.ds(pl.multiple_of(vlm_rows + s * ar, ar), ar), s)

    step = 32
    v0, a0, _ = place(p, m)

    @pl.loop(0, vr // step)
    def _(i):
        o = pl.multiple_of(i * step, step)
        tok[pl.ds(pl.multiple_of((p * mp_size + m) * vr + o, step), step), :] = normalize(
            vlm_ref[pl.ds(o, step), :], gain_ref[...])

    @pl.loop(0, ar // step)
    def _(i):
        o = pl.multiple_of(i * step, step)
        tok[pl.ds(pl.multiple_of(vlm_rows + (p * mp_size + m) * ar + o, step), step), :] = normalize(
            act_ref[pl.ds(o, step), :], gain_ref[...])

    pl.semaphore_wait(barrier, 3 + has_left.astype(jnp.int32) + has_right.astype(jnp.int32))

    def w_copy(block, k, side, own=False):
        rows = pl.ds(pl.multiple_of(block * r, r), r)
        cc = pl.ds(pl.multiple_of(k * cw, cw), cw)
        return pltpu.make_async_remote_copy(
            src_ref=proj_ref.at[:, cc] if own else wbuf.at[rows, cc],
            dst_ref=wbuf.at[rows, cc],
            send_sem=w_send.at[side, block, k],
            recv_sem=w_recv.at[block, k],
            device_id=(d - 2 if side == 0 else d + 2, m),
            device_id_type=MESH,
        )

    def send_w(block, k, own=False):
        @pl.when(has_left & (block >= g))
        def _():
            w_copy(block, k, 0, own).start()

        @pl.when(has_right & (block <= g))
        def _():
            w_copy(block, k, 1, own).start()

    for k in range(chunks):
        send_w(g, k, True)

    def tok_copies(pp, mm, to, slot):
        va, aa, s = place(pp, mm)
        return [pltpu.make_async_remote_copy(
            src_ref=tok.at[rows, :], dst_ref=tok.at[rows, :], send_sem=tok_send.at[slot, j],
            recv_sem=tok_recv.at[s, j], device_id=to, device_id_type=MESH)
            for j, rows in enumerate((va, aa))]

    def tok_start(pp, mm, to, slot):
        for copy in tok_copies(pp, mm, to, slot):
            copy.start()

    def tok_arrive(pp, mm):
        for copy in tok_copies(pp, mm, sibling, 0):
            copy.wait_recv()

    m_y = (1 - y) * 2 + c
    m_s = y * 2 + 1 - c
    m_ys = (1 - y) * 2 + 1 - c
    tok_start(p, m, xpart, 0)
    tok_start(p, m, ypart, 1)
    tok_start(p, m, sibling, 2)

    given = pl.multiple_of((1 - p) * half, half)
    ex = pltpu.make_async_remote_copy(
        src_ref=proj_ref.at[pl.ds(given, half), :],
        dst_ref=new_out.at[:, pl.ds(pl.multiple_of(p * cols, cols), cols)],
        send_sem=ex_send, recv_sem=ex_recv, device_id=xpart, device_id_type=MESH)
    ex.start()
    load_w().wait()
    kept = pltpu.make_async_copy(
        wbuf.at[pl.ds(pl.multiple_of(g * r + p * half, half), half), :],
        new_out.at[:, pl.ds(pl.multiple_of(p * cols, cols), cols)], loc.at[1])
    kept.start()

    tok_arrive(1 - p, m)
    tok_start(1 - p, m, ypart, 3)
    tok_start(1 - p, m, sibling, 4)

    def arrive(s, k):
        @pl.when(g - s >= 0)
        def _():
            w_copy(g - s, k, 1).wait_recv()
            send_w(g - s, k)

        @pl.when(g + s < groups)
        def _():
            w_copy(g + s, k, 0).wait_recv()
            send_w(g + s, k)

    def phase(s):
        @pl.loop(0, chunks)
        def _(k):
            arrive(s, k)

    if groups > 2:
        phase(1)
    tok_arrive(p, m_y)
    tok_start(p, m_y, sibling, 5)
    tok_arrive(1 - p, m_y)
    tok_start(1 - p, m_y, sibling, 6)
    if groups > 3:
        @pl.loop(2, groups - 1)
        def _(s):
            phase(s)
    for pp, mm in ((p, m_s), (1 - p, m_s), (p, m_ys), (1 - p, m_ys)):
        tok_arrive(pp, mm)

    def hid_copy(k):
        cc = pl.ds(pl.multiple_of(k * cw, cw), cw)
        oc = pl.ds(pl.multiple_of(p * cols + k * cw, cw), cw)
        return pltpu.make_async_remote_copy(
            src_ref=hid.at[pl.ds(pl.multiple_of(vlm_rows + (1 - p) * act_rows, act_rows), act_rows), cc],
            dst_ref=act_out.at[:, oc], send_sem=hid_send.at[k], recv_sem=hid_recv.at[k],
            device_id=xpart, device_id_type=MESH)

    def hid_back(k):
        oc = pl.ds(pl.multiple_of((1 - p) * cols + k * cw, cw), cw)
        return pltpu.make_async_remote_copy(
            src_ref=act_out.at[:, oc], dst_ref=act_out.at[:, oc], send_sem=hid_send.at[k],
            recv_sem=hid_recv.at[k], device_id=xpart, device_id_type=MESH)

    def own_copies(k):
        cc = pl.ds(pl.multiple_of(k * cw, cw), cw)
        oc = pl.ds(pl.multiple_of(p * cols + k * cw, cw), cw)
        return (
            pltpu.make_async_copy(
                hid.at[pl.ds(pl.multiple_of(vlm_rows + p * act_rows, act_rows), act_rows), cc],
                act_out.at[:, oc], loc.at[2 + 2 * k]),
            pltpu.make_async_copy(hid.at[pl.ds(0, vlm_rows), cc], vlm_out.at[:, cc], loc.at[3 + 2 * k]))

    tile = math.gcd(256, math.gcd(vlm_rows, act_rows))

    def compute(first, count, k):
        cc = pl.ds(pl.multiple_of(k * cw, cw), cw)

        @pl.loop(0, count // tile)
        def _(t):
            rows = pl.ds(pl.multiple_of(first + t * tile, tile), tile)
            pre = jnp.dot(tok[rows, :], wbuf[:, cc], preferred_element_type=jnp.float32)
            hid[rows, cc] = gelu(pre)

    @pl.loop(0, chunks)
    def _(k):
        if groups > 1:
            arrive(groups - 1, k)
        compute(vlm_rows + (1 - p) * act_rows, act_rows, k)
        hid_copy(k).start()
        compute(vlm_rows + p * act_rows, act_rows, k)
        own_copies(k)[0].start()
        compute(0, vlm_rows, k)
        own_copies(k)[1].start()

    to_of = ((p, m, xpart), (p, m, ypart), (p, m, sibling), (1 - p, m, ypart), (1 - p, m, sibling),
             (p, m_y, sibling), (1 - p, m_y, sibling))
    for slot, (pp, mm, to) in enumerate(to_of):
        for copy in tok_copies(pp, mm, to, slot):
            copy.wait_send()

    @pl.loop(0, groups)
    def _(block):
        @pl.loop(0, chunks)
        def _(k):
            @pl.when(has_left & (block >= g))
            def _():
                w_copy(block, k, 0).wait_send()

            @pl.when(has_right & (block <= g))
            def _():
                w_copy(block, k, 1).wait_send()

    ex.wait_send()
    pltpu.make_async_remote_copy(
        src_ref=proj_ref.at[pl.ds(given, half), :],
        dst_ref=new_out.at[:, pl.ds(pl.multiple_of((1 - p) * cols, cols), cols)],
        send_sem=ex_send, recv_sem=ex_recv, device_id=xpart, device_id_type=MESH).wait_recv()
    kept.wait()

    @pl.loop(0, chunks)
    def _(k):
        for copy in own_copies(k):
            copy.wait()
        hid_copy(k).wait_send()
        hid_back(k).wait_recv()


def solution(mesh):
    groups, mp_size = mesh.shape["dp"] // 2, mesh.shape["mp"]

    def local(vlm_tokens, action_tokens, norm_gain, proj_old):
        vr, ar = vlm_tokens.shape[0], action_tokens.shape[0]
        features = vlm_tokens.shape[1]
        r, cols = proj_old.shape
        vlm_rows, act_rows = 2 * mp_size * vr, mp_size * ar
        bf16 = jnp.bfloat16
        dma = pltpu.SemaphoreType.DMA
        vmem, hbm = pl.BlockSpec(memory_space=pltpu.VMEM), pl.BlockSpec(memory_space=pl.ANY)
        return pl.pallas_call(
            functools.partial(kernel, groups, mp_size, CHUNKS),
            name="up_gelu",
            out_shape=(
                jax.ShapeDtypeStruct((vlm_rows, cols), bf16),
                jax.ShapeDtypeStruct((act_rows, 2 * cols), bf16),
                jax.ShapeDtypeStruct((r // 2, 2 * cols), bf16),
            ),
            in_specs=[vmem, vmem, vmem, hbm],
            out_specs=(hbm, hbm, hbm),
            scratch_shapes=[
                pltpu.VMEM((vlm_rows + 2 * act_rows, features), bf16),
                pltpu.VMEM((groups * r, cols), bf16),
                pltpu.VMEM((vlm_rows + 2 * act_rows, cols), bf16),
                dma((7, 2)), dma((2 * mp_size, 2)),
                dma((2, groups, CHUNKS)), dma((groups, CHUNKS)),
                dma, dma, dma((CHUNKS,)), dma((CHUNKS,)), dma((2 + 2 * CHUNKS,)),
            ],
            compiler_params=pltpu.CompilerParams(
                collective_id=0, has_side_effects=True, vmem_limit_bytes=48 * 1024 * 1024),
        )(vlm_tokens, action_tokens, norm_gain.reshape(1, -1), proj_old)

    return jax.shard_map(
        local,
        mesh=mesh,
        in_specs=(P(("dp", "mp"), None), P(("dp", "mp"), None), P(), P("dp", "mp")),
        out_specs=(P("dp", "mp"), P("dp", "mp"), P("dp", "mp")),
        check_vma=False,
    )
```

time: 211 us -> 89.4 us (0.42)
  waiting for transfers between devices: 140 us -> 0 us
  Pallas kernels: 0 us -> 81.3 us
  matrix products: 27.9 us -> 0 us
  between operations: 14.1 us -> 0.65 us
  starting transfers between devices: 12.3 us -> 0 us
  other arithmetic: 10.2 us -> 0 us
    ppermute x4 -> x0, waiting for transfers between devices: 102 us -> none  [partner(): lax.ppermute(array, axis, [(i, i ^ 1 << apart) for i in range(lax.axis_si...]
    pallas_call x0 -> x1, Pallas kernels: none -> 81.3 us  [local(): pl.pallas_call(functools.partial(kernel, groups, mp_size, CHUNKS), name='...]
    all_gather x2 -> x0, waiting for transfers between devices: 36.2 us -> none  [the longest x1 24.9 us: local(): action_rows = lax.all_gather(action_tokens, 'mp', axis=0, tiled=True)]
    dot_general x2 -> x0, matrix products: 27.9 us -> none  [the longest x1 18.1 us: local(): jnp.dot(both_rows, own_weight, preferred_element_type=jnp.float32)]
    all_to_all x1 -> x0, starting transfers between devices: 6.19 us -> none  [local(): lax.all_to_all(tiled_halves, 'dp', split_axis=0, concat_axis=0, tiled=True)]
    ppermute x4 -> x0, starting transfers between devices: 6.04 us -> none  [partner(): lax.ppermute(array, axis, [(i, i ^ 1 << apart) for i in range(lax.axis_si...]
    unnamed x3 -> x11, local copies, waits for them, and re-layouts: 2.38 us -> 7.17 us
    convert_element_type x1 -> x0, other arithmetic: 3.45 us -> none  [normalize(): return (values * factor * norm_gain).astype(jnp.bfloat16)]
  transfers between devices with their start and end apart: 7 -> 0, of which waited for: 5 -> 0; matrix products, arithmetic and copies ran while one was open for 9% -> 0% of each run, Pallas kernels for 0% -> 0%
where the time goes in v1:
time: 89.4 us; the launch traced here: 89.1 us
  Pallas kernels  81.3 us (91%)
  local copies, waits for them, and re-layouts  7.17 us (8%)
    pallas_call x1, Pallas kernels, local(): pl.pallas_call(functools.partial(kernel, groups, mp_size, CHUNKS), name='...  81.3 us
    unnamed x11, local copies, waits for them, and re-layouts  7.17 us

profile of v1, /device:TPU:0, one launch (start us, length us, event | category | flops | bytes accessed | tf_op | source)
XLA Modules:
  0.0 89.1 jit_solution(7818850203352820460)
XLA Ops:
  0.6 0.0 copy-start
  0.6 1.2 %copy-done = bf16[512,1024]{1,0:T(8,128)(2,1)S(1)} copy-done((bf16[512,1024]{1,0:T(8,128)(2,1)S(1)}, bf16[512,1024]{1,0:T(8,128)(2,1)}, u32[]{:S(2)}) %copy-start) | copy-done | bytes 1048600
  1.9 0.0 copy-start.1
  1.9 1.0 %copy-done.1 = bf16[128,2048]{1,0:T(8,128)(2,1)S(1)} copy-done((bf16[128,2048]{1,0:T(8,128)(2,1)S(1)}, bf16[128,2048]{1,0:T(8,128)(2,1)}, u32[]{:S(2)}) %copy-start.1) | copy-done | bytes 524312
  2.9 0.0 copy-start.2
  2.9 0.9 %copy-done.2 = bf16[64,2048]{1,0:T(8,128)(2,1)S(1)} copy-done((bf16[64,2048]{1,0:T(8,128)(2,1)S(1)}, bf16[64,2048]{1,0:T(8,128)(2,1)}, u32[]{:S(2)}) %copy-start.2) | copy-done | bytes 262168
  3.8 0.0 copy-start.3
  3.9 0.7 copy-done.3
  4.5 81.3 %up_gelu.1 = (bf16[512,1024]{1,0:T(8,128)(2,1)S(1)}, bf16[512,2048]{1,0:T(8,128)(2,1)S(1)}, bf16[256,2048]{1,0:T(8,128)(2,1)S(1)}) custom-call(bf16[64,2048]{1,0:T(8,128)(2,1)S(1)} %copy-done.2, bf16[128,2048]{1,0:T(8,128)(2,1)S(1)} %copy-done.1, f32[1,2048]{1,0:T(1,128)S(1)} %bitcast.1, bf16[512,1024]{1,0:T(8,128)(2,1)S(1)} %copy-done), custom_call_target="tpu_custom_call" | custom-call | tf_op jit(solution)/shard_map/up_gelu/pallas_call | solution.py:259
  85.8 1.0 %copy.10 = bf16[512,1024]{1,0:T(8,128)(2,1)} copy(bf16[512,1024]{1,0:T(8,128)(2,1)S(1)} %get-tuple-element.6) | data formatting | bytes 2097152
  86.8 1.3 %copy.11 = bf16[512,2048]{1,0:T(8,128)(2,1)} copy(bf16[512,2048]{1,0:T(8,128)(2,1)S(1)} %get-tuple-element.7) | data formatting | bytes 4194304
  88.1 1.0 %copy.12 = bf16[256,2048]{1,0:T(8,128)(2,1)} copy(bf16[256,2048]{1,0:T(8,128)(2,1)S(1)} %get-tuple-element.8) | data formatting | bytes 2097152
Async XLA Ops:
  0.6 1.2 %copy-start = (bf16[512,1024]{1,0:T(8,128)(2,1)S(1)}, bf16[512,1024]{1,0:T(8,128)(2,1)}, u32[]{:S(2)}) copy-start(bf16[512,1024]{1,0:T(8,128)(2,1)} %proj_ref.1) | copy-start | bytes 3145732
  1.9 1.0 %copy-start.1 = (bf16[128,2048]{1,0:T(8,128)(2,1)S(1)}, bf16[128,2048]{1,0:T(8,128)(2,1)}, u32[]{:S(2)}) copy-start(bf16[128,2048]{1,0:T(8,128)(2,1)} %act_ref.1) | copy-start | bytes 1572868
  2.9 0.9 %copy-start.2 = (bf16[64,2048]{1,0:T(8,128)(2,1)S(1)}, bf16[64,2048]{1,0:T(8,128)(2,1)}, u32[]{:S(2)}) copy-start(bf16[64,2048]{1,0:T(8,128)(2,1)} %vlm_ref.1) | copy-start | bytes 786436
  3.8 0.7 copy-start.3

commit v2 on v1

v2 whole, which is shorter than its diff:
```python
import functools
import math
import jax
import jax.numpy as jnp
from jax import lax
from jax.experimental import pallas as pl
from jax.experimental.pallas import tpu as pltpu
from jax.sharding import PartitionSpec as P

MESH = pl.DeviceIdType.MESH
epsilon = 1e-06


def column_plan(cols):
    wide = cols // 4
    narrow = max(wide // 2, 128)
    return ((0, wide, 3, 0), (3 * wide, narrow, wide // narrow, 3))


def number_of_chunks(cols):
    return sum(count for _, _, count, _ in column_plan(cols))


def normalize(row_values, norm_gain):
    values = row_values.astype(jnp.float32)
    factor = lax.rsqrt(jnp.mean(values * values, axis=-1, keepdims=True) + epsilon)
    return (values * factor * norm_gain).astype(jnp.bfloat16)


def gelu(u):
    return (u * 0.5 * (1.0 + lax.erf(u * math.sqrt(0.5)))).astype(jnp.bfloat16)


def kernel(groups, mp_size, vlm_hbm, act_hbm, gain_hbm, proj_hbm, vlm_out, act_out, new_out,
           vlm_ref, act_ref, gain_ref, tok, wbuf, hid, tok_send, tok_recv, w_send, w_recv, ex_send, ex_recv, hid_send, hid_recv, loc, load_sem,
           own_sem, vlm_sem):
    d = lax.axis_index("dp")
    m = lax.axis_index("mp")
    g, p = d // 2, d % 2
    y, c = m // 2, m % 2
    vr, ar = vlm_ref.shape[0], act_ref.shape[0]
    r, cols = proj_hbm.shape
    half = r // 2
    plan = column_plan(cols)
    vlm_rows, act_rows = 2 * mp_size * vr, mp_size * ar
    sibling = (d, y * 2 + 1 - c)
    xpart = (g * 2 + 1 - p, m)
    ypart = (d, (1 - y) * 2 + c)
    has_left, has_right = g > 0, g < groups - 1

    barrier = pltpu.get_barrier_semaphore()
    for other in (sibling, xpart, ypart):
        pl.semaphore_signal(barrier, inc=1, device_id=other, device_id_type=MESH)

    @pl.when(has_left)
    def _():
        pl.semaphore_signal(barrier, inc=1, device_id=(d - 2, m), device_id_type=MESH)

    @pl.when(has_right)
    def _():
        pl.semaphore_signal(barrier, inc=1, device_id=(d + 2, m), device_id_type=MESH)

    def load_w():
        return pltpu.make_async_copy(proj_hbm, wbuf.at[pl.ds(pl.multiple_of(g * r, r), r), :], loc.at[0])

    loads = [pltpu.make_async_copy(src, dst, load_sem.at[i]) for i, (src, dst) in enumerate(
        ((gain_hbm, gain_ref), (vlm_hbm, vlm_ref), (act_hbm, act_ref)))]
    load_w().start()
    for load in loads:
        load.start()
    pl.semaphore_wait(barrier, 3 + has_left.astype(jnp.int32) + has_right.astype(jnp.int32))
    load_w().wait()

    def each_chunk(body):
        for first, width, count, base in plan:
            @pl.loop(0, count)
            def _(i):
                body(pl.ds(pl.multiple_of(first + i * width, width), width), base + i)

    def w_copy(block, cc, k, side):
        rows = pl.ds(pl.multiple_of(block * r, r), r)
        return pltpu.make_async_remote_copy(
            src_ref=wbuf.at[rows, cc],
            dst_ref=wbuf.at[rows, cc],
            send_sem=w_send.at[side, block, k],
            recv_sem=w_recv.at[block, k],
            device_id=(d - 2 if side == 0 else d + 2, m),
            device_id_type=MESH,
        )

    def send_w(block, cc, k):
        @pl.when(has_left & (block >= g))
        def _():
            w_copy(block, cc, k, 0).start()

        @pl.when(has_right & (block <= g))
        def _():
            w_copy(block, cc, k, 1).start()

    each_chunk(lambda cc, k: send_w(g, cc, k))
    for load in loads:
        load.wait()

    def place(pp, mm):
        s = pp * mp_size + mm
        return (pl.ds(pl.multiple_of(s * vr, vr), vr), pl.ds(pl.multiple_of(vlm_rows + s * ar, ar), ar), s)

    step = 32

    @pl.loop(0, vr // step)
    def _(i):
        o = pl.multiple_of(i * step, step)
        tok[pl.ds(pl.multiple_of((p * mp_size + m) * vr + o, step), step), :] = normalize(
            vlm_ref[pl.ds(o, step), :], gain_ref[...])

    @pl.loop(0, ar // step)
    def _(i):
        o = pl.multiple_of(i * step, step)
        tok[pl.ds(pl.multiple_of(vlm_rows + (p * mp_size + m) * ar + o, step), step), :] = normalize(
            act_ref[pl.ds(o, step), :], gain_ref[...])

    def tok_copies(pp, mm, to, slot):
        va, aa, s = place(pp, mm)
        return [pltpu.make_async_remote_copy(
            src_ref=tok.at[rows, :], dst_ref=tok.at[rows, :], send_sem=tok_send.at[slot, j],
            recv_sem=tok_recv.at[s, j], device_id=to, device_id_type=MESH)
            for j, rows in enumerate((va, aa))]

    def tok_start(pp, mm, to, slot):
        for copy in tok_copies(pp, mm, to, slot):
            copy.start()

    def tok_arrive(pp, mm):
        for copy in tok_copies(pp, mm, sibling, 0):
            copy.wait_recv()

    m_y = (1 - y) * 2 + c
    m_s = y * 2 + 1 - c
    m_ys = (1 - y) * 2 + 1 - c
    tok_start(p, m, xpart, 0)
    tok_start(p, m, ypart, 1)
    tok_start(p, m, sibling, 2)

    ex = pltpu.make_async_remote_copy(
        src_ref=wbuf.at[pl.ds(pl.multiple_of(g * r + (1 - p) * half, half), half), :],
        dst_ref=new_out.at[:, pl.ds(pl.multiple_of(p * cols, cols), cols)],
        send_sem=ex_send, recv_sem=ex_recv, device_id=xpart, device_id_type=MESH)
    ex.start()
    kept = pltpu.make_async_copy(
        wbuf.at[pl.ds(pl.multiple_of(g * r + p * half, half), half), :],
        new_out.at[:, pl.ds(pl.multiple_of(p * cols, cols), cols)], loc.at[1])
    kept.start()

    tok_arrive(1 - p, m)
    tok_start(1 - p, m, ypart, 3)
    tok_start(1 - p, m, sibling, 4)

    def arrive(s, cc, k):
        @pl.when(g - s >= 0)
        def _():
            w_copy(g - s, cc, k, 1).wait_recv()
            send_w(g - s, cc, k)

        @pl.when(g + s < groups)
        def _():
            w_copy(g + s, cc, k, 0).wait_recv()
            send_w(g + s, cc, k)

    def phase(s):
        each_chunk(lambda cc, k: arrive(s, cc, k))

    if groups > 2:
        phase(1)
    tok_arrive(p, m_y)
    tok_start(p, m_y, sibling, 5)
    tok_arrive(1 - p, m_y)
    tok_start(1 - p, m_y, sibling, 6)
    if groups > 3:
        @pl.loop(2, groups - 1)
        def _(s):
            phase(s)
    for pp, mm in ((p, m_s), (1 - p, m_s), (p, m_ys), (1 - p, m_ys)):
        tok_arrive(pp, mm)

    tile = math.gcd(256, math.gcd(vlm_rows, act_rows))
    a_tiles, v_tiles = act_rows // tile, vlm_rows // tile

    def out_cols(side, cc):
        return pl.ds(pl.multiple_of(side * cols + cc.start, cc.size), cc.size)

    def tile_rows(start):
        return pl.ds(pl.multiple_of(start, tile), tile)

    def hid_copy(cc, k, t):
        return pltpu.make_async_remote_copy(
            src_ref=hid.at[tile_rows(vlm_rows + (1 - p) * act_rows + t * tile), cc],
            dst_ref=act_out.at[tile_rows(t * tile), out_cols(p, cc)],
            send_sem=hid_send.at[k, t], recv_sem=hid_recv.at[k, t], device_id=xpart, device_id_type=MESH)

    def hid_back(cc, k, t):
        there = act_out.at[tile_rows(t * tile), out_cols(1 - p, cc)]
        return pltpu.make_async_remote_copy(
            src_ref=there, dst_ref=there, send_sem=hid_send.at[k, t], recv_sem=hid_recv.at[k, t],
            device_id=xpart, device_id_type=MESH)

    def own_copy(cc, k):
        return pltpu.make_async_copy(
            hid.at[pl.ds(pl.multiple_of(vlm_rows + p * act_rows, act_rows), act_rows), cc],
            act_out.at[:, out_cols(p, cc)], own_sem.at[k])

    def vlm_copy(cc, k):
        return pltpu.make_async_copy(hid.at[pl.ds(0, vlm_rows), cc], vlm_out.at[:, cc], vlm_sem.at[k])

    def compute(cc, k):
        if groups > 1:
            arrive(groups - 1, cc, k)

        @pl.loop(0, 2 * a_tiles + v_tiles)
        def _(t):
            start = jnp.where(
                t < a_tiles, vlm_rows + (1 - p) * act_rows + t * tile,
                jnp.where(t < 2 * a_tiles, vlm_rows + p * act_rows + (t - a_tiles) * tile, (t - 2 * a_tiles) * tile))
            rows = tile_rows(start)
            pre = jnp.dot(tok[rows, :], wbuf[:, cc], preferred_element_type=jnp.float32)
            hid[rows, cc] = gelu(pre)

            @pl.when(t < a_tiles)
            def _():
                hid_copy(cc, k, t).start()

            @pl.when(t == 2 * a_tiles - 1)
            def _():
                own_copy(cc, k).start()

        vlm_copy(cc, k).start()

    each_chunk(compute)

    to_of = ((p, m, xpart), (p, m, ypart), (p, m, sibling), (1 - p, m, ypart), (1 - p, m, sibling),
             (p, m_y, sibling), (1 - p, m_y, sibling))
    for slot, (pp, mm, to) in enumerate(to_of):
        for copy in tok_copies(pp, mm, to, slot):
            copy.wait_send()

    @pl.loop(0, groups)
    def _(block):
        def sent(cc, k):
            @pl.when(has_left & (block >= g))
            def _():
                w_copy(block, cc, k, 0).wait_send()

            @pl.when(has_right & (block <= g))
            def _():
                w_copy(block, cc, k, 1).wait_send()

        each_chunk(sent)

    ex.wait_send()
    taken = new_out.at[:, pl.ds(pl.multiple_of((1 - p) * cols, cols), cols)]
    pltpu.make_async_remote_copy(
        src_ref=taken, dst_ref=taken, send_sem=ex_send, recv_sem=ex_recv,
        device_id=xpart, device_id_type=MESH).wait_recv()
    kept.wait()

    def finish(cc, k):
        own_copy(cc, k).wait()
        vlm_copy(cc, k).wait()

        @pl.loop(0, a_tiles)
        def _(t):
            hid_copy(cc, k, t).wait_send()
            hid_back(cc, k, t).wait_recv()

    each_chunk(finish)


def store(*refs):
    count = (len(refs) - 1) // 2
    copies = [pltpu.make_async_copy(refs[i], refs[count + i], refs[-1].at[i]) for i in range(count)]
    for copy in copies:
        copy.start()
    for copy in copies:
        copy.wait()


def solution(mesh):
    groups, mp_size = mesh.shape["dp"] // 2, mesh.shape["mp"]

    def local(vlm_tokens, action_tokens, norm_gain, proj_old):
        vr, ar = vlm_tokens.shape[0], action_tokens.shape[0]
        features = vlm_tokens.shape[1]
        r, cols = proj_old.shape
        vlm_rows, act_rows = 2 * mp_size * vr, mp_size * ar
        bf16 = jnp.bfloat16
        dma = pltpu.SemaphoreType.DMA
        hbm, anywhere = pl.BlockSpec(memory_space=pltpu.HBM), pl.BlockSpec(memory_space=pl.ANY)
        chunks = number_of_chunks(cols)
        a_tiles = act_rows // math.gcd(256, math.gcd(vlm_rows, act_rows))
        shapes = (
            jax.ShapeDtypeStruct((vlm_rows, cols), bf16),
            jax.ShapeDtypeStruct((act_rows, 2 * cols), bf16),
            jax.ShapeDtypeStruct((r // 2, 2 * cols), bf16),
        )
        results = pl.pallas_call(
            functools.partial(kernel, groups, mp_size),
            name="up_gelu",
            out_shape=shapes,
            in_specs=[hbm] * 4,
            out_specs=(anywhere,) * 3,
            scratch_shapes=[
                pltpu.VMEM((vr, features), bf16),
                pltpu.VMEM((ar, features), bf16),
                pltpu.VMEM((1, features), jnp.float32),
                pltpu.VMEM((vlm_rows + 2 * act_rows, features), bf16),
                pltpu.VMEM((groups * r, cols), bf16),
                pltpu.VMEM((vlm_rows + 2 * act_rows, cols), bf16),
                dma((7, 2)), dma((2 * mp_size, 2)),
                dma((2, groups, chunks)), dma((groups, chunks)),
                dma, dma, dma((chunks, a_tiles)), dma((chunks, a_tiles)), dma((2,)), dma((3,)),
                dma((chunks,)), dma((chunks,)),
            ],
            compiler_params=pltpu.CompilerParams(
                collective_id=0, has_side_effects=True, vmem_limit_bytes=48 * 1024 * 1024),
        )(*[pltpu.with_memory_space_constraint(array, pltpu.HBM) for array in (
            vlm_tokens, action_tokens, norm_gain.reshape(1, -1), proj_old)])
        return pl.pallas_call(
            store,
            name="store",
            out_shape=shapes,
            in_specs=[anywhere] * 3,
            out_specs=(hbm,) * 3,
            scratch_shapes=[dma((3,))],
            compiler_params=pltpu.CompilerParams(vmem_limit_bytes=1024 * 1024),
        )(*results)

    return jax.shard_map(
        local,
        mesh=mesh,
        in_specs=(P(("dp", "mp"), None), P(("dp", "mp"), None), P(), P("dp", "mp")),
        out_specs=(P("dp", "mp"), P("dp", "mp"), P("dp", "mp")),
        check_vma=False,
    )
```

time: 89.4 us -> 84 us (0.940)
  local copies, waits for them, and re-layouts: 7.17 us -> 0 us
  Pallas kernels: 81.3 us -> 83.2 us
    unnamed x11 -> x0, local copies, waits for them, and re-layouts: 7.17 us -> none
    pallas_call x1 -> x2, Pallas kernels: 81.3 us -> 83.2 us  [the longest x1 81.2 us: local(): pl.pallas_call(functools.partial(kernel, groups, mp_size), name='up_gelu'...]
where the time goes in v2:
time: 84 us; the launch traced here: 83.8 us
  Pallas kernels  83.2 us (99%)
    pallas_call x1, Pallas kernels, local(): pl.pallas_call(functools.partial(kernel, groups, mp_size), name='up_gelu'...  81.2 us
    pallas_call x1, Pallas kernels, local(): pl.pallas_call(store, name='store', out_shape=shapes, in_specs=[anywhere]...  2.03 us

profile of v2, /device:TPU:0, one launch (start us, length us, event | category | flops | bytes accessed | tf_op | source)
XLA Modules:
  0.0 83.8 jit_solution(8848849875983199602)
XLA Ops:
  0.6 81.2 %up_gelu.1 = (bf16[512,1024]{1,0:T(8,128)(2,1)S(1)}, bf16[512,2048]{1,0:T(8,128)(2,1)S(1)}, bf16[256,2048]{1,0:T(8,128)(2,1)S(1)}) custom-call(bf16[64,2048]{1,0:T(8,128)(2,1)} %vlm_hbm.1, bf16[128,2048]{1,0:T(8,128)(2,1)} %act_hbm.1, f32[1,2048]{1,0:T(1,128)} %bitcast.1, bf16[512,1024]{1,0:T(8,128)(2,1)} %proj_hbm.1), custom_call_target="tpu_custom_call" | custom-call | tf_op jit(solution)/shard_map/up_gelu/pallas_call | solution.py:304
  81.8 2.0 %store.1 = (bf16[512,1024]{1,0:T(8,128)(2,1)}, bf16[512,2048]{1,0:T(8,128)(2,1)}, bf16[256,2048]{1,0:T(8,128)(2,1)}) custom-call(bf16[512,1024]{1,0:T(8,128)(2,1)S(1)} %get-tuple-element.6.refs_0_, bf16[512,2048]{1,0:T(8,128)(2,1)S(1)} %get-tuple-element.7.refs_1_, bf16[256,2048]{1,0:T(8,128)(2,1)S(1)} %get-tuple-element.8.refs_2_), custom_call_target="tpu_custom_call" | custom-call | tf_op jit(solution)/shard_map/store/pallas_call | solution.py:326

commit v3 on v2

--- a/solution.py
+++ b/solution.py
@@ -33,7 +33,7 @@
 
 def kernel(groups, mp_size, vlm_hbm, act_hbm, gain_hbm, proj_hbm, vlm_out, act_out, new_out,
            vlm_ref, act_ref, gain_ref, tok, wbuf, hid, tok_send, tok_recv, w_send, w_recv, ex_send, ex_recv, hid_send, hid_recv, loc, load_sem,
-           own_sem, vlm_sem):
+           own_sem, vlm_sem, loc_w):
     d = lax.axis_index("dp")
     m = lax.axis_index("mp")
     g, p = d // 2, d % 2
@@ -48,9 +48,13 @@
     ypart = (d, (1 - y) * 2 + c)
     has_left, has_right = g > 0, g < groups - 1
 
+    def each_chunk(body, parts=plan):
+        for first, width, count, base in parts:
+            @pl.loop(0, count)
+            def _(i):
+                body(pl.ds(pl.multiple_of(first + i * width, width), width), base + i)
+
     barrier = pltpu.get_barrier_semaphore()
-    for other in (sibling, xpart, ypart):
-        pl.semaphore_signal(barrier, inc=1, device_id=other, device_id_type=MESH)
 
     @pl.when(has_left)
     def _():
@@ -60,22 +64,19 @@
     def _():
         pl.semaphore_signal(barrier, inc=1, device_id=(d + 2, m), device_id_type=MESH)
 
-    def load_w():
-        return pltpu.make_async_copy(proj_hbm, wbuf.at[pl.ds(pl.multiple_of(g * r, r), r), :], loc.at[0])
+    for other in (xpart, ypart, sibling):
+        pl.semaphore_signal(barrier, inc=1, device_id=other, device_id_type=MESH)
+
+    def load_w(cc, k):
+        return pltpu.make_async_copy(
+            proj_hbm.at[:, cc], wbuf.at[pl.ds(pl.multiple_of(g * r, r), r), cc], loc_w.at[k])
 
     loads = [pltpu.make_async_copy(src, dst, load_sem.at[i]) for i, (src, dst) in enumerate(
         ((gain_hbm, gain_ref), (vlm_hbm, vlm_ref), (act_hbm, act_ref)))]
-    load_w().start()
+    each_chunk(lambda cc, k: load_w(cc, k).start())
     for load in loads:
         load.start()
     pl.semaphore_wait(barrier, 3 + has_left.astype(jnp.int32) + has_right.astype(jnp.int32))
-    load_w().wait()
-
-    def each_chunk(body):
-        for first, width, count, base in plan:
-            @pl.loop(0, count)
-            def _(i):
-                body(pl.ds(pl.multiple_of(first + i * width, width), width), base + i)
 
     def w_copy(block, cc, k, side):
         rows = pl.ds(pl.multiple_of(block * r, r), r)
@@ -97,7 +98,11 @@
         def _():
             w_copy(block, cc, k, 1).start()
 
-    each_chunk(lambda cc, k: send_w(g, cc, k))
+    def send_own(cc, k):
+        load_w(cc, k).wait()
+        send_w(g, cc, k)
+
+    each_chunk(send_own)
     for load in loads:
         load.wait()
 
@@ -148,12 +153,8 @@
     ex.start()
     kept = pltpu.make_async_copy(
         wbuf.at[pl.ds(pl.multiple_of(g * r + p * half, half), half), :],
-        new_out.at[:, pl.ds(pl.multiple_of(p * cols, cols), cols)], loc.at[1])
+        new_out.at[:, pl.ds(pl.multiple_of(p * cols, cols), cols)], loc)
     kept.start()
-
-    tok_arrive(1 - p, m)
-    tok_start(1 - p, m, ypart, 3)
-    tok_start(1 - p, m, sibling, 4)
 
     def arrive(s, cc, k):
         @pl.when(g - s >= 0)
@@ -166,11 +167,16 @@
             w_copy(g + s, cc, k, 0).wait_recv()
             send_w(g + s, cc, k)
 
-    def phase(s):
-        each_chunk(lambda cc, k: arrive(s, cc, k))
+    def phase(s, parts=plan):
+        each_chunk(lambda cc, k: arrive(s, cc, k), parts)
 
     if groups > 2:
-        phase(1)
+        phase(1, plan[:1])
+    tok_arrive(1 - p, m)
+    tok_start(1 - p, m, ypart, 3)
+    tok_start(1 - p, m, sibling, 4)
+    if groups > 2:
+        phase(1, plan[1:])
     tok_arrive(p, m_y)
     tok_start(p, m_y, sibling, 5)
     tok_arrive(1 - p, m_y)
@@ -316,8 +322,8 @@
                 pltpu.VMEM((vlm_rows + 2 * act_rows, cols), bf16),
                 dma((7, 2)), dma((2 * mp_size, 2)),
                 dma((2, groups, chunks)), dma((groups, chunks)),
-                dma, dma, dma((chunks, a_tiles)), dma((chunks, a_tiles)), dma((2,)), dma((3,)),
-                dma((chunks,)), dma((chunks,)),
+                dma, dma, dma((chunks, a_tiles)), dma((chunks, a_tiles)), dma, dma((3,)),
+                dma((chunks,)), dma((chunks,)), dma((chunks,)),
             ],
             compiler_params=pltpu.CompilerParams(
                 collective_id=0, has_side_effects=True, vmem_limit_bytes=48 * 1024 * 1024),

time: 84 us -> 84 us (level)
  no operation moved by 1% of the time
where the time goes in v3:
time: 84 us; the launch traced here: 83.8 us
  Pallas kernels  83.2 us (99%)
    pallas_call x1, Pallas kernels, local(): pl.pallas_call(functools.partial(kernel, groups, mp_size), name='up_gelu'...  81.1 us
    pallas_call x1, Pallas kernels, local(): pl.pallas_call(store, name='store', out_shape=shapes, in_specs=[anywhere]...  2.03 us

profile of v3, /device:TPU:0, one launch (start us, length us, event | category | flops | bytes accessed | tf_op | source)
XLA Modules:
  0.0 83.8 jit_solution(15658904119244813794)
XLA Ops:
  0.6 81.1 %up_gelu.1 = (bf16[512,1024]{1,0:T(8,128)(2,1)S(1)}, bf16[512,2048]{1,0:T(8,128)(2,1)S(1)}, bf16[256,2048]{1,0:T(8,128)(2,1)S(1)}) custom-call(bf16[64,2048]{1,0:T(8,128)(2,1)} %vlm_hbm.1, bf16[128,2048]{1,0:T(8,128)(2,1)} %act_hbm.1, f32[1,2048]{1,0:T(1,128)} %bitcast.1, bf16[512,1024]{1,0:T(8,128)(2,1)} %proj_hbm.1), custom_call_target="tpu_custom_call" | custom-call | tf_op jit(solution)/shard_map/up_gelu/pallas_call | solution.py:310
  81.8 2.0 %store.1 = (bf16[512,1024]{1,0:T(8,128)(2,1)}, bf16[512,2048]{1,0:T(8,128)(2,1)}, bf16[256,2048]{1,0:T(8,128)(2,1)}) custom-call(bf16[512,1024]{1,0:T(8,128)(2,1)S(1)} %get-tuple-element.6.refs_0_, bf16[512,2048]{1,0:T(8,128)(2,1)S(1)} %get-tuple-element.7.refs_1_, bf16[256,2048]{1,0:T(8,128)(2,1)S(1)} %get-tuple-element.8.refs_2_), custom_call_target="tpu_custom_call" | custom-call | tf_op jit(solution)/shard_map/store/pallas_call | solution.py:332

commit v4 on v3

--- a/solution.py
+++ b/solution.py
@@ -217,30 +217,40 @@
     def vlm_copy(cc, k):
         return pltpu.make_async_copy(hid.at[pl.ds(0, vlm_rows), cc], vlm_out.at[:, cc], vlm_sem.at[k])
 
-    def compute(cc, k):
+    def hidden(rows, cc):
+        pre = jnp.dot(tok[rows, :], wbuf[:, cc], preferred_element_type=jnp.float32)
+        hid[rows, cc] = gelu(pre)
+
+    def for_partner(cc, k):
         if groups > 1:
             arrive(groups - 1, cc, k)
 
-        @pl.loop(0, 2 * a_tiles + v_tiles)
+        @pl.loop(0, a_tiles)
         def _(t):
-            start = jnp.where(
-                t < a_tiles, vlm_rows + (1 - p) * act_rows + t * tile,
-                jnp.where(t < 2 * a_tiles, vlm_rows + p * act_rows + (t - a_tiles) * tile, (t - 2 * a_tiles) * tile))
-            rows = tile_rows(start)
-            pre = jnp.dot(tok[rows, :], wbuf[:, cc], preferred_element_type=jnp.float32)
-            hid[rows, cc] = gelu(pre)
-
-            @pl.when(t < a_tiles)
-            def _():
-                hid_copy(cc, k, t).start()
-
-            @pl.when(t == 2 * a_tiles - 1)
+            hidden(tile_rows(vlm_rows + (1 - p) * act_rows + t * tile), cc)
+            hid_copy(cc, k, t).start()
+
+    def for_self(cc, k):
+        @pl.loop(0, a_tiles + v_tiles)
+        def _(t):
+            hidden(tile_rows(jnp.where(
+                t < a_tiles, vlm_rows + p * act_rows + t * tile, (t - a_tiles) * tile)), cc)
+
+            @pl.when(t == a_tiles - 1)
             def _():
                 own_copy(cc, k).start()
 
         vlm_copy(cc, k).start()
 
-    each_chunk(compute)
+    def for_both(cc, k):
+        for_partner(cc, k)
+        for_self(cc, k)
+
+    first, width, count, base = plan[1]
+    merged = ((first, width * count, 1, base),)
+    each_chunk(for_both, plan[:1])
+    each_chunk(for_partner, plan[1:])
+    each_chunk(for_self, merged)
 
     to_of = ((p, m, xpart), (p, m, ypart), (p, m, sibling), (1 - p, m, ypart), (1 - p, m, sibling),
              (p, m_y, sibling), (1 - p, m_y, sibling))
@@ -269,14 +279,16 @@
     kept.wait()
 
     def finish(cc, k):
-        own_copy(cc, k).wait()
-        vlm_copy(cc, k).wait()
-
         @pl.loop(0, a_tiles)
         def _(t):
             hid_copy(cc, k, t).wait_send()
             hid_back(cc, k, t).wait_recv()
 
+    def stored(cc, k):
+        own_copy(cc, k).wait()
+        vlm_copy(cc, k).wait()
+
+    each_chunk(stored, plan[:1] + merged)
     each_chunk(finish)
 
 

time: 84 us -> 83.9 us (level)
  no operation moved by 1% of the time
where the time goes in v4:
time: 83.9 us; the launch traced here: 83.8 us
  Pallas kernels  83.2 us (99%)
    pallas_call x1, Pallas kernels, local(): pl.pallas_call(functools.partial(kernel, groups, mp_size), name='up_gelu'...  81.1 us
    pallas_call x1, Pallas kernels, local(): pl.pallas_call(store, name='store', out_shape=shapes, in_specs=[anywhere]...  2.03 us

profile of v4, /device:TPU:0, one launch (start us, length us, event | category | flops | bytes accessed | tf_op | source)
XLA Modules:
  0.0 83.8 jit_solution(17218352338595203863)
XLA Ops:
  0.6 81.1 %up_gelu.1 = (bf16[512,1024]{1,0:T(8,128)(2,1)S(1)}, bf16[512,2048]{1,0:T(8,128)(2,1)S(1)}, bf16[256,2048]{1,0:T(8,128)(2,1)S(1)}) custom-call(bf16[64,2048]{1,0:T(8,128)(2,1)} %vlm_hbm.1, bf16[128,2048]{1,0:T(8,128)(2,1)} %act_hbm.1, f32[1,2048]{1,0:T(1,128)} %bitcast.1, bf16[512,1024]{1,0:T(8,128)(2,1)} %proj_hbm.1), custom_call_target="tpu_custom_call" | custom-call | tf_op jit(solution)/shard_map/up_gelu/pallas_call | solution.py:322
  81.8 2.0 %store.1 = (bf16[512,1024]{1,0:T(8,128)(2,1)}, bf16[512,2048]{1,0:T(8,128)(2,1)}, bf16[256,2048]{1,0:T(8,128)(2,1)}) custom-call(bf16[512,1024]{1,0:T(8,128)(2,1)S(1)} %get-tuple-element.6.refs_0_, bf16[512,2048]{1,0:T(8,128)(2,1)S(1)} %get-tuple-element.7.refs_1_, bf16[256,2048]{1,0:T(8,128)(2,1)S(1)} %get-tuple-element.8.refs_2_), custom_call_target="tpu_custom_call" | custom-call | tf_op jit(solution)/shard_map/store/pallas_call | solution.py:344
